TPU v7x, 128 devices: a whole 4x4x4 slice. The times are simulated.
128 devices in a mesh: cuts: 8 (over z, x_lo), row: 16 (over x_hi, y, core).
Axes of the slice: x: 4 (x_hi: 2, x_lo: 2; x = x_hi * 2 + x_lo), y: 4, z: 4, core: 2. Of those that a mesh axis runs over, the one named last changes fastest.
Arguments:
- eigvecs: float32 [16384, 4096], P('row', 'cuts'), may hold values from -1.2 to 1.2
- slice_counts: int32 [8], P('cuts'), may hold values from 256 to 512, as said below
- occ_index: int32 [4096], P('cuts'), may hold values from 0 to 63
- occ_levels: float32 [64], replicated, may hold values from 0 to 1
Outputs:
- slab: float32 [4096, 16384], P('cuts', 'row')
Inputs may be any that keep to these rules, and one draw needn't show every extreme that they name: `slice_counts`: some slice holds exactly 512 eigenvalues in every draw; the others at least half of that.
All inputs are finite; a program needn't handle non-finite values.
Results may differ from a plain program's by a relative error of at most 0.000062.
Values sent between devices are 32-bit elements; how exact they have to be, the bound alone decides.
A program may use at most 128 MiB of HBM per device.

v0:
```python
import jax
import jax.numpy as jnp
from jax import lax
from jax.sharding import Mesh
from jax.sharding import PartitionSpec as P

BLOCK = 1024
SLAB_SUB = 256
CUTS = ("cuts_0", "cuts_1")


def sum_by_axis(total, axes):
    for axis in axes:
        total = lax.psum_scatter(total, axis, scatter_dimension=0, tiled=True)
    return total


def shards(eigvecs, slice_counts, occ_index, occ_levels):
    row_count = eigvecs.shape[0]
    slot_count = eigvecs.shape[1]
    level_ids = jnp.arange(occ_levels.shape[0], dtype=jnp.int32)
    one_hot = (occ_index[:, None] == level_ids[None, :]).astype(jnp.float32)
    values = jnp.dot(one_hot, occ_levels, precision=lax.Precision.HIGHEST)
    live = jnp.arange(slot_count, dtype=jnp.int32) < slice_counts[0]
    weights = jnp.where(live, values, jnp.float32(0.0))
    local_blocks = eigvecs.reshape(row_count // BLOCK, BLOCK, slot_count)[:, :SLAB_SUB, :]
    local_rows = local_blocks.reshape(-1, slot_count) * weights[None, :]
    gathered = lax.all_gather(local_rows, "row", axis=0, tiled=True)
    return sum_by_axis(
        lax.dot_general(
            gathered,
            eigvecs,
            (((1,), (1,)), ((), ())),
            precision=lax.Precision.HIGHEST,
            preferred_element_type=jnp.float32,
        ),
        CUTS,
    )


def solution(mesh):
    finer = Mesh(mesh.devices.reshape(4, 2, mesh.shape["row"]), ("cuts_0", "cuts_1", "row"))
    in_specs = (P("row", CUTS), P(CUTS), P(CUTS), P())
    out_specs = P(CUTS, "row")
    return jax.shard_map(
        shards, mesh=finer, in_specs=in_specs, out_specs=out_specs, check_vma=False
    )
```

profile of v0, /device:TPU:1, one launch (start us, length us, event | category | flops | bytes accessed | tf_op | source)
XLA Modules:
  0.0 329.1 jit_solution(11867658746482311696)
XLA Ops:
  6.5 0.0 copy-start
  6.5 0.0 all-gather.2.cloned.1.call-start
  7.2 0.0 copy-done
  7.2 1.0 fusion.1
  8.2 1.9 fusion
  10.1 0.0 all-gather.2.cloned.1.call-update
  10.1 0.0 reduce-scatter.3.cloned.1.call-start
  10.2 76.3 %all-gather.2.cloned.1.call-done = f32[4096,512]{1,0:T(8,128)} async-done(((f32[256,512]{1,0:T(8,128)}), f32[4096,512]{1,0:T(8,128)}) %all-gather.2.cloned.1.call-update) | async-done | bytes 8388624 | tf_op jit(solution)/shard_map/all_gather | solution.py:28
  86.4 31.7 %fusion.5 = f32[4096,1024]{1,0:T(8,128)} fusion(f32[4096,512]{1,0:T(8,128)} %all-gather.2.cloned.1.call-done, f32[1024,512]{1,0:T(8,128)} %param.4), kind=kOutput, calls=%fused_computation.8 | convolution fusion | flops 25769803776 | bytes 27262976 | tf_op jit(solution)/shard_map/dot_general | solution.py:30
  118.1 0.0 reduce-scatter.3.cloned.1.call-update
  118.1 0.0 reduce-scatter.5.cloned.1.call-start
  118.2 145.6 %reduce-scatter.3.cloned.1.call-done = f32[1024,1024]{1,0:T(8,128)} async-done(((f32[4096,1024]{1,0:T(8,128)}), f32[1024,1024]{1,0:T(8,128)}) %reduce-scatter.3.cloned.1.call-update) | async-done | bytes 4194320 | tf_op jit(solution)/shard_map/reduce_scatter | solution.py:14
  263.8 0.0 reduce-scatter.5.cloned.1.call-update
  263.8 58.8 %reduce-scatter.5.cloned.1.call-done = f32[512,1024]{1,0:T(8,128)} async-done(((f32[1024,1024]{1,0:T(8,128)}), f32[512,1024]{1,0:T(8,128)}) %reduce-scatter.5.cloned.1.call-update) | async-done | bytes 2097168 | tf_op jit(solution)/shard_map/reduce_scatter | solution.py:14
  (1 shorter events, 0.0 us)
Async XLA Ops:
  6.5 0.7 copy-start
  6.5 79.9 %all-gather.2.cloned.1.call-start = ((), (), s32[]{:S(2)}) async-start(), calls=%async_computation.2 | async-start | bytes 8912896 | tf_op jit(solution)/shard_map/all_gather | solution.py:28
  10.1 253.7 %reduce-scatter.3.cloned.1.call-start = ((), (), s32[]{:S(2)}) async-start(), calls=%async_computation.3 | async-start | bytes 20971520 | tf_op jit(solution)/shard_map/reduce_scatter | solution.py:14
  118.1 204.5 %reduce-scatter.5.cloned.1.call-start = ((), (), s32[]{:S(2)}) async-start(), calls=%async_computation.4 | async-start | bytes 6291456 | tf_op jit(solution)/shard_map/reduce_scatter | solution.py:14
Sparse Core Ops, SparseCore 0:
  10.2 76.1 all-gather.1
  118.3 145.5 reduce-scatter.2
  266.2 56.3 reduce-scatter.4
where the time goes:
time: 329 us
  waiting for transfers between devices  281 us (85%)
  matrix products  32.7 us (10%)
  between operations  13.8 us (4%)
    reduce_scatter x2, waiting for transfers between devices, sum_by_axis(): total = lax.psum_scatter(total, axis, scatter_dimension=0, tiled=True)  204 us
    all_gather x1, waiting for transfers between devices, shards(): gathered = lax.all_gather(local_rows, 'row', axis=0, tiled=True)  76.3 us
    dot_general x1, matrix products, shards(): lax.dot_general(gathered, eigvecs, (((1,), (1,)), ((), ())), precision=la...  31.7 us
  transfers between devices with their start and end apart: 3, of which 3 were waited for; matrix products, arithmetic and copies ran while one was open for 0% of the time, Pallas kernels for 0%

commit v1 on v0

--- a/solution.py
+++ b/solution.py
@@ -25,7 +25,9 @@
     weights = jnp.where(live, values, jnp.float32(0.0))
     local_blocks = eigvecs.reshape(row_count // BLOCK, BLOCK, slot_count)[:, :SLAB_SUB, :]
     local_rows = local_blocks.reshape(-1, slot_count) * weights[None, :]
-    gathered = lax.all_gather(local_rows, "row", axis=0, tiled=True)
+    gathered = jnp.concatenate(
+        lax.all_to_all(jnp.stack([local_rows] * lax.axis_size("row")), "row", 0, 0), 0
+    )
     return sum_by_axis(
         lax.dot_general(
             gathered,

time: 329 us -> 357 us (1.085)
  blocking collectives: 0 us -> 104 us
  waiting for transfers between devices: 281 us -> 206 us
    all_to_all x0 -> x1, blocking collectives: none -> 104 us  [shards(): lax.all_to_all(jnp.stack([local_rows] * lax.axis_size('row')), 'row', 0, 0)]
    all_gather x1 -> x0, waiting for transfers between devices: 76.3 us -> none  [shards(): gathered = lax.all_gather(local_rows, 'row', axis=0, tiled=True)]
  transfers between devices with their start and end apart: 3 -> 2, of which waited for: 3 -> 2; matrix products, arithmetic and copies ran while one was open for 0% -> 0% of each run, Pallas kernels for 0% -> 0%
where the time goes in v1:
time: 357 us
  waiting for transfers between devices  206 us (58%)
  blocking collectives  104 us (29%)
  matrix products  30.9 us (9%)
  between operations  14.1 us (4%)
    reduce_scatter x2, waiting for transfers between devices, sum_by_axis(): total = lax.psum_scatter(total, axis, scatter_dimension=0, tiled=True)  206 us
    all_to_all x1, blocking collectives, shards(): lax.all_to_all(jnp.stack([local_rows] * lax.axis_size('row')), 'row', 0, 0)  104 us
    dot_general x1, matrix products, shards(): lax.dot_general(gathered, eigvecs, (((1,), (1,)), ((), ())), precision=la...  29.9 us
  transfers between devices with their start and end apart: 2, of which 2 were waited for; matrix products, arithmetic and copies ran while one was open for 0% of the time, Pallas kernels for 0%

profile of v1, /device:TPU:1, one launch (start us, length us, event | category | flops | bytes accessed | tf_op | source)
XLA Modules:
  0.0 357.2 jit_solution(1778164764065327968)
XLA Ops:
  6.5 0.0 copy-start
  6.5 0.0 reduce-scatter.3.cloned.1.call-start
  7.2 0.0 copy-done
  7.2 1.0 fusion.1
  8.2 1.1 fusion
  9.3 1.1 stack.5
  10.4 0.0 copy-start.1
  10.4 103.8 %all_to_all.5 = f32[16,256,512]{2,1,0:T(8,128)S(1)} all-to-all(f32[16,256,512]{2,1,0:T(8,128)S(1)} %stack.5), channel_id=1, replica_groups=mesh['cuts_0'=4,'cuts_1'=2,'row'=16] {'row'}, dimensions={0} | all-to-all | bytes 16777216 | tf_op jit(solution)/shard_map/all_to_all | solution.py:29
  114.2 0.0 copy-done.1
  114.2 29.9 %fusion.5 = f32[4096,1024]{1,0:T(8,128)} fusion(f32[4096,512]{1,0:T(8,128)S(1)} %bitcast.12, f32[1024,512]{1,0:T(8,128)S(1)} %copy-done.1), kind=kOutput, calls=%fused_computation.8 | convolution fusion | flops 25769803776 | bytes 27262976 | tf_op jit(solution)/shard_map/dot_general | solution.py:32
  144.1 0.0 reduce-scatter.3.cloned.1.call-update
  144.1 0.0 reduce-scatter.5.cloned.1.call-start
  144.2 147.4 %reduce-scatter.3.cloned.1.call-done = f32[1024,1024]{1,0:T(8,128)} async-done(((f32[4096,1024]{1,0:T(8,128)}), f32[1024,1024]{1,0:T(8,128)}) %reduce-scatter.3.cloned.1.call-update) | async-done | bytes 4194320 | tf_op jit(solution)/shard_map/reduce_scatter | solution.py:14
  291.5 0.0 reduce-scatter.5.cloned.1.call-update
  291.6 58.8 %reduce-scatter.5.cloned.1.call-done = f32[512,1024]{1,0:T(8,128)} async-done(((f32[1024,1024]{1,0:T(8,128)}), f32[512,1024]{1,0:T(8,128)}) %reduce-scatter.5.cloned.1.call-update) | async-done | bytes 2097168 | tf_op jit(solution)/shard_map/reduce_scatter | solution.py:14
  (1 shorter events, 0.0 us)
Async XLA Ops:
  6.5 0.7 copy-start
  6.5 285.0 %reduce-scatter.3.cloned.1.call-start = ((), (), s32[]{:S(2)}) async-start(), calls=%async_computation.3 | async-start | bytes 20971520 | tf_op jit(solution)/shard_map/reduce_scatter | solution.py:14
  10.4 103.8 %copy-start.1 = (f32[1024,512]{1,0:T(8,128)S(1)}, f32[1024,512]{1,0:T(8,128)}, u32[]{:S(2)}) copy-start(f32[1024,512]{1,0:T(8,128)} %param.4) | copy-start | bytes 6291460
  144.1 206.2 %reduce-scatter.5.cloned.1.call-start = ((), (), s32[]{:S(2)}) async-start(), calls=%async_computation.4 | async-start | bytes 6291456 | tf_op jit(solution)/shard_map/reduce_scatter | solution.py:14
Sparse Core Ops, SparseCore 0:
  144.2 147.2 reduce-scatter.2
  293.9 56.3 reduce-scatter.4
